TPU v7x, 32 devices: a whole 2x2x4 slice. The times are simulated.
32 devices in a mesh: row: 8 (over y, x, core), col: 4 (over z).
Axes of the slice: x: 2, y: 2, z: 4, core: 2. Of those that a mesh axis runs over, the one named last changes fastest.
Arguments:
- slc_stack: float32 [20, 2, 64, 512], P(None, None, 'row', 'col'), may hold values from -6 to 6
- land_mask: int32 [64, 512], P('row', 'col'), may hold values from 0 to 1, as said below
Outputs:
- linked: float32 [20, 2, 64, 512], P(None, None, 'row', 'col')
- compressed_final: float32 [2, 64, 512], P(None, 'row', 'col')
- mean_strength: float32 [2], replicated
Inputs may be any that keep to these rules, and one draw needn't show every extreme that they name: `land_mask`: 1 marks a valid pixel, 0 a water pixel.
All inputs are finite; a program needn't handle non-finite values.
Results may differ from a plain program's by a relative error of at most 0.00012.
Values sent between devices are 32-bit elements; how exact they have to be, the bound alone decides.
A program may use at most 64 MiB of HBM per device.

v0:
```python
import functools

import jax
import jax.numpy as jnp
from jax import lax
from jax.experimental import pallas as pl
from jax.experimental.pallas import tpu as pltpu
from jax.sharding import PartitionSpec as P

M = 10
MS = 2
WIN = 11
ITERS = 4
REACH = WIN // 2
SUB = 8

covariance_floor = 8.0

AROUND = ((-1, 0), (1, 0), (-1, -1), (0, -1), (1, -1), (-1, 1), (0, 1), (1, 1))
SLOTS = M + SUB
HALO_ROWS = 24
HALO_ROOM = 40


def fresh_units():
    units = [((0, 0, 0), (SUB, 0, 0))]
    for lag in range(1, M):
        for first in range(0, M - lag, SUB):
            units.append(((first, lag, 0), (first, lag, 1)))
    return units


def field_of(units):
    table = {}
    for index, unit in enumerate(units):
        for half, (first, lag, part) in enumerate(unit):
            for lane in range(SUB):
                i = first + lane
                if i + lag < M:
                    table[(i, i + lag, part)] = index * 2 * SUB + half * SUB + lane
    return table


FRESH = fresh_units()
FIELDS = field_of(FRESH)


def window_sums(lines, outputs):
    core = lines[outputs - 1]
    for e in range(outputs, WIN):
        core = core + lines[e]
    low = [None] * outputs
    low[outputs - 1] = core
    for r in range(outputs - 2, -1, -1):
        low[r] = low[r + 1] + lines[r]
    sums = [low[0]]
    high = None
    for r in range(1, outputs):
        extra = lines[WIN - 1 + r]
        high = extra if high is None else high + extra
        sums.append(low[r] + high)
    return sums


def split(value):
    high = value.astype(jnp.bfloat16)
    low = (value - high.astype(jnp.float32)).astype(jnp.bfloat16)
    return high, low


def kernel(
    row_count,
    col_count,
    slc,
    land,
    linked,
    comp_out,
    strength,
    sig,
    up,
    dn,
    pack_send,
    pack_recv,
    halo,
    comp_send,
    comp_up,
    comp_dn,
    cpack_send,
    cpack_recv,
    w_main,
    w_halo,
    ybuf,
    hbuf,
    zbuf,
    ycbuf,
    hcbuf,
    zcbuf,
    coh,
    part,
    red_row,
    red_col,
    send_a,
    recv_a,
    send_b,
    recv_b,
    send_r,
    recv_r,
    send_c,
    recv_c,
):
    rows, cols = land.shape
    my_row = lax.axis_index("row")
    my_col = lax.axis_index("col")
    strip = rows * REACH

    exists = []
    for dr, dc in AROUND:
        ok = None
        for pos, step, count in ((my_row, dr, row_count), (my_col, dc, col_count)):
            if step:
                here = (pos > 0) if step < 0 else (pos < count - 1)
                ok = here if ok is None else jnp.logical_and(ok, here)
        exists.append(ok)

    for k, (dr, dc) in enumerate(AROUND):

        @pl.when(jnp.logical_not(exists[k]))
        def _(k=k, dc=dc, dr=dr):
            if dc == 0:
                target, small = (up, comp_up) if dr < 0 else (dn, comp_dn)
                for m in range(MS):
                    target[m] = jnp.zeros(target.shape[1:], jnp.float32)
                small[...] = jnp.zeros_like(small)
            else:
                for m in range(MS):
                    pack_recv[m, k - 2] = jnp.zeros(pack_recv.shape[2:], jnp.float32)
                cpack_recv[k - 2] = jnp.zeros(cpack_recv.shape[1:], jnp.float32)

    barrier = pltpu.get_barrier_semaphore()
    mesh_id = pl.DeviceIdType.MESH
    expected = jnp.int32(row_count - 1 + col_count - 1)
    for step in range(1, row_count):
        pl.semaphore_signal(
            barrier, inc=1, device_id=(lax.rem(my_row + step, row_count), my_col), device_id_type=mesh_id
        )
    for step in range(1, col_count):
        pl.semaphore_signal(
            barrier, inc=1, device_id=(my_row, lax.rem(my_col + step, col_count)), device_id_type=mesh_id
        )
    for k, (dr, dc) in enumerate(AROUND):
        if dr and dc:

            @pl.when(exists[k])
            def _(dr=dr, dc=dc):
                pl.semaphore_signal(
                    barrier, inc=1, device_id=(my_row + dr, my_col + dc), device_id_type=mesh_id
                )

            expected = expected + exists[k].astype(jnp.int32)

    mask = land[...].astype(jnp.float32)
    for m in range(MS):
        for i in range(M):
            for c in range(2):
                at = (i * 2 + c) * rows
                sig[m, at : at + rows, :] = slc[m * M + i, c] * mask
        for buffer in (sig, up, dn):
            buffer[m, M * 2 * rows :, :] = jnp.zeros((buffer.shape[1] - M * 2 * rows, cols), jnp.float32)

    lane = lax.broadcasted_iota(jnp.int32, (rows, cols), 1)
    sub = lax.broadcasted_iota(jnp.int32, (rows, cols), 0)
    from_right = (lane >= sub * REACH) & (lane < sub * REACH + REACH)
    from_left = (lane >= (sub + 1) * REACH) & (lane < (sub + 2) * REACH)

    def pack_tile(tile):
        turned = pltpu.roll(tile, REACH, 1, stride=REACH, stride_axis=0)
        high = jnp.sum(jnp.where(from_right, turned, 0.0), axis=0, keepdims=True)
        low = jnp.sum(jnp.where(from_left, turned, 0.0), axis=0, keepdims=True)
        return low, high

    def spread(line, shift):
        total = pltpu.roll(line, cols - shift, 1) if shift else line
        return (
            total
            + pltpu.roll(line, (strip - shift) % cols, 1)
            + pltpu.roll(line, (2 * strip - shift) % cols, 1)
        )

    for m in range(MS):
        pack_send[m] = jnp.zeros(pack_send.shape[1:], jnp.float32)
        for i in range(M):
            for c in range(2):
                low, high = pack_tile(sig[m, (i * 2 + c) * rows : (i * 2 + c + 1) * rows, :])
                pack_send[m, 0, c * (M + 1) + i : c * (M + 1) + i + 1, :] = low
                pack_send[m, 1, c * (M + 1) + i : c * (M + 1) + i + 1, :] = high
        pack_send[m, 0] = spread(pack_send[m, 0], REACH)
        pack_send[m, 1] = spread(pack_send[m, 1], 0)
        pack_recv[m, :, HALO_ROWS:, :] = jnp.zeros((6, HALO_ROOM - HALO_ROWS, cols), jnp.float32)

    pl.semaphore_wait(barrier, expected)

    def mirror(k):
        dr, dc = AROUND[k]
        return AROUND.index((-dr, -dc))

    def fresh_copy(m, k):
        dr, dc = AROUND[k]
        back = mirror(k)
        if dc == 0:
            source = sig.at[m, pl.ds(0, M * 2 * rows)]
            target = (dn if dr < 0 else up).at[m, pl.ds(0, M * 2 * rows)]
        else:
            source = pack_send.at[m, 0 if dc < 0 else 1]
            target = pack_recv.at[m, back - 2, pl.ds(0, HALO_ROWS)]
        return pltpu.make_async_remote_copy(
            src_ref=source,
            dst_ref=target,
            send_sem=send_a.at[m, k],
            recv_sem=recv_a.at[m, back],
            device_id=(my_row + dr, my_col + dc),
            device_id_type=mesh_id,
        )

    def fresh_arrival(m, k):
        dr, dc = AROUND[k]
        if dc == 0:
            source = sig.at[m, pl.ds(0, M * 2 * rows)]
            target = (up if dr < 0 else dn).at[m, pl.ds(0, M * 2 * rows)]
        else:
            source = pack_send.at[m, 0 if dc < 0 else 1]
            target = pack_recv.at[m, k - 2, pl.ds(0, HALO_ROWS)]
        return pltpu.make_async_remote_copy(
            src_ref=source,
            dst_ref=target,
            send_sem=send_a.at[m, k],
            recv_sem=recv_a.at[m, k],
            device_id=(my_row + dr, my_col + dc),
            device_id_type=mesh_id,
        )

    def each_around(action):
        for k in range(len(AROUND)):

            @pl.when(exists[k])
            def _(k=k):
                action(k)

    for m in range(MS):
        each_around(lambda k, m=m: fresh_copy(m, k).start())

    k_at = lax.broadcasted_iota(jnp.int32, (cols, cols), 0)
    n_at = lax.broadcasted_iota(jnp.int32, (cols, cols), 1)
    near = jnp.where((k_at - n_at <= REACH) & (n_at - k_at <= REACH), 1.0, 0.0).astype(jnp.bfloat16)
    w_main[0:cols, :] = near
    w_main[cols:, :] = near
    line_of = k_at // REACH
    inner = k_at - line_of * REACH
    for side in range(2):
        touches = (n_at <= inner) if side == 0 else (n_at >= inner + cols - REACH)
        line = jnp.where(touches, line_of, -1)
        for r in range(rows):
            first = rows - REACH + r
            w_halo[side * cols : (side + 1) * cols, r * cols : (r + 1) * cols] = jnp.where(
                (line >= first) & (line < first + WIN), 1.0, 0.0
            ).astype(jnp.bfloat16)

    outer = (up, sig, dn)
    lane_halo = lax.broadcasted_iota(jnp.int32, (HALO_ROOM, cols), 1)

    def gather_halo(m, parts, target):
        for side in range(2):
            a, b, c = (parts(side * 3 + j) for j in range(3))
            which = lane_halo[: a.shape[0]]
            target(side, jnp.where(which < strip, a, jnp.where(which < 2 * strip, b, c)))

    def line_tile(m, e, c, first):
        at = rows - REACH + e
        buffer = outer[at // rows]
        return buffer[m, pl.ds((first * 2 + c) * rows + at % rows, SUB, stride=2 * rows), :]

    def halo_tile(m, side, c, first):
        at = c * (M + 1) + first
        return halo[m, side, at : at + SUB, :]

    def emit(index, halves, ytarget, htarget):
        lines_total = WIN + rows - 1
        both = [jnp.concatenate([x, y], 0) for x, y in zip(halves[0], halves[1])]
        at = slice(index * 2 * SUB, (index + 1) * 2 * SUB)
        for r, total in enumerate(window_sums(both[:lines_total], rows)):
            high, low = split(total)
            ytarget[r, at, 0:cols] = high
            ytarget[r, at, cols:] = low
        for side in range(2):
            high, low = split(both[lines_total + side])
            htarget[0, at, side * cols : (side + 1) * cols] = high
            htarget[1, at, side * cols : (side + 1) * cols] = low

    def sources(m):
        lines_total = WIN + rows - 1
        return [functools.partial(line_tile, m, e) for e in range(lines_total)] + [
            functools.partial(halo_tile, m, side) for side in range(2)
        ]

    def real_part(a, b, x, y):
        return a * x + b * y

    def imag_part(a, b, x, y):
        return b * x - a * y

    def fresh_fields(m):
        for index, unit in enumerate(FRESH):
            halves = ([], [])
            for tile in sources(m):
                if index == 0:
                    for half in range(2):
                        first = unit[half][0]
                        a, b = tile(0, first), tile(1, first)
                        halves[half].append(a * a + b * b)
                else:
                    first, lag, _ = unit[0]
                    a, b = tile(0, first), tile(1, first)
                    x, y = tile(0, first + lag), tile(1, first + lag)
                    halves[0].append(real_part(a, b, x, y))
                    halves[1].append(imag_part(a, b, x, y))
            emit(index, halves, ybuf, hbuf)

    def windowed(ysource, hsource, target):
        count = ysource.shape[1]
        main = jnp.dot(
            ysource[...].reshape(rows * count, 2 * cols), w_main[...], preferred_element_type=jnp.float32
        )
        for r in range(rows):
            band = w_halo[:, r * cols : (r + 1) * cols]
            edge = jnp.dot(hsource[0], band, preferred_element_type=jnp.float32) + jnp.dot(
                hsource[1], band, preferred_element_type=jnp.float32
            )
            target[r * count : (r + 1) * count, :] = main[r * count : (r + 1) * count, :] + edge

    fresh_count = len(FRESH) * 2 * SUB

    def fresh_field(i, j, p):
        return zbuf[pl.ds(FIELDS[(i, j, p)], rows, stride=fresh_count), :]

    def power(number, field):
        scales = [
            lax.rsqrt(jnp.maximum(field(i, i, 0), covariance_floor)) for i in range(number)
        ]
        vec_re = [None] * number
        vec_im = [None] * number

        def add(store, i, value):
            store[i] = value if store[i] is None else store[i] + value

        def sub_(store, i, value):
            store[i] = -value if store[i] is None else store[i] - value

        slot = {}
        next_slot = 0
        for i in range(number):
            c = field(i, i, 0) * (scales[i] * scales[i])
            coh[next_slot] = c
            slot[(i, i, 0)] = next_slot
            next_slot += 1
            add(vec_re, i, c)
            for j in range(i + 1, number):
                s = scales[i] * scales[j]
                c = field(i, j, 0) * s
                d = field(i, j, 1) * s
                coh[next_slot] = c
                coh[next_slot + 1] = d
                slot[(i, j, 0)] = next_slot
                slot[(i, j, 1)] = next_slot + 1
                next_slot += 2
                add(vec_re, i, c)
                add(vec_re, j, c)
                add(vec_im, i, d)
                sub_(vec_im, j, d)

        def normalise():
            squares = None
            for i in range(number):
                both = vec_re[i] * vec_re[i] + vec_im[i] * vec_im[i]
                squares = both if squares is None else squares + both
            length = jnp.sqrt(squares)
            inverse = 1.0 / jnp.maximum(length, 1.0)
            return length, [v * inverse for v in vec_re], [v * inverse for v in vec_im]

        length, old_re, old_im = normalise()
        for _ in range(1, ITERS):
            vec_re = [None] * number
            vec_im = [None] * number
            for i in range(number):
                c = coh[slot[(i, i, 0)]]
                add(vec_re, i, c * old_re[i])
                add(vec_im, i, c * old_im[i])
                for j in range(i + 1, number):
                    c = coh[slot[(i, j, 0)]]
                    d = coh[slot[(i, j, 1)]]
                    add(vec_re, i, c * old_re[j] - d * old_im[j])
                    add(vec_im, i, c * old_im[j] + d * old_re[j])
                    add(vec_re, j, c * old_re[i] + d * old_im[i])
                    add(vec_im, j, c * old_im[i] - d * old_re[i])
            length, old_re, old_im = normalise()
        return length, old_re, old_im

    def finish(m, number, field):
        length, re, im = power(number, field)
        re, im = re[number - M :], im[number - M :]
        comp_re = comp_im = None
        for i in range(M):
            a = sig[m, i * 2 * rows : (i * 2 + 1) * rows, :]
            b = sig[m, (i * 2 + 1) * rows : (i * 2 + 2) * rows, :]
            x = re[i] * a + im[i] * b
            y = re[i] * b - im[i] * a
            comp_re = x if comp_re is None else comp_re + x
            comp_im = y if comp_im is None else comp_im + y
            linked[m * M + i, 0] = re[i] * mask
            linked[m * M + i, 1] = im[i] * mask
        part[m : m + 1, :] = jnp.sum(mask * length, axis=0, keepdims=True) * (1.0 / number)
        return comp_re, comp_im

    def take_fresh(m):
        each_around(lambda k: fresh_arrival(m, k).wait_recv())

        def put(side, value):
            halo[m, side] = value

        gather_halo(m, lambda j: pack_recv[m, j], put)

    take_fresh(0)
    fresh_fields(0)
    windowed(ybuf, hbuf, zbuf)
    comp_re, comp_im = finish(0, M, fresh_field)
    comp_send[0:rows, :] = comp_re
    comp_send[rows:, :] = comp_im
    cpack_send[...] = jnp.zeros_like(cpack_send)
    for c, value in enumerate((comp_re, comp_im)):
        low, high = pack_tile(value)
        cpack_send[0, c : c + 1, :] = spread(low, REACH)
        cpack_send[1, c : c + 1, :] = spread(high, 0)

    def comp_pair(k, sending):
        dr, dc = AROUND[k]
        slot = mirror(k) if sending else k
        if dc == 0:
            source = comp_send
            target = comp_up if AROUND[slot][0] < 0 else comp_dn
        else:
            source = cpack_send.at[0 if dc < 0 else 1]
            target = cpack_recv.at[slot - 2]
        return pltpu.make_async_remote_copy(
            src_ref=source,
            dst_ref=target,
            send_sem=send_b.at[k],
            recv_sem=recv_b.at[slot],
            device_id=(my_row + dr, my_col + dc),
            device_id_type=mesh_id,
        )

    each_around(lambda k: comp_pair(k, True).start())

    last = MS - 1
    take_fresh(last)
    fresh_fields(last)
    windowed(ybuf, hbuf, zbuf)

    each_around(lambda k: comp_pair(k, False).wait_recv())
    at = M * 2 * rows
    sig[last, at : at + 2 * rows, :] = comp_send[...]
    up[last, at : at + 2 * rows, :] = comp_up[...]
    dn[last, at : at + 2 * rows, :] = comp_dn[...]

    def put_comp(side, value):
        for c in range(2):
            row = c * (M + 1) + M
            halo[last, side, row : row + 1, :] = value[c : c + 1]

    gather_halo(last, lambda j: cpack_recv[j], put_comp)

    for index, first in enumerate(range(0, M + 1, SUB)):
        halves = ([], [])
        for tile_at in range(WIN + rows - 1 + 2):
            if tile_at < WIN + rows - 1:
                pos = rows - REACH + tile_at
                buffer = outer[pos // rows]
                base = M * 2 * rows + pos % rows
                a = buffer[last, base : base + 1, :]
                b = buffer[last, base + rows : base + rows + 1, :]
            else:
                side = tile_at - (WIN + rows - 1)
                a = halo[last, side, M : M + 1, :]
                b = halo[last, side, 2 * M + 1 : 2 * M + 2, :]
            a = jnp.broadcast_to(a, (SUB, cols))
            b = jnp.broadcast_to(b, (SUB, cols))
            tile = sources(last)[tile_at]
            x, y = tile(0, first), tile(1, first)
            halves[0].append(real_part(a, b, x, y))
            halves[1].append(imag_part(a, b, x, y))
        emit(index, halves, ycbuf, hcbuf)
    windowed(ycbuf, hcbuf, zcbuf)
    comp_count = ycbuf.shape[1]

    def last_field(i, j, p):
        if i > 0:
            return fresh_field(i - 1, j - 1, p)
        other = M if j == 0 else j - 1
        at = (other // SUB) * 2 * SUB + p * SUB + other % SUB
        return zcbuf[pl.ds(at, rows, stride=comp_count), :]

    part[...] = jnp.where(lax.broadcasted_iota(jnp.int32, part.shape, 0) < 1, part[...], 0.0)
    comp_re, comp_im = finish(last, M + 1, last_field)
    comp_out[0] = comp_re
    comp_out[1] = comp_im

    def reduce(count, me, device, source, buffer, sends, recvs):
        copies = []
        for step in range(1, count):
            copy = pltpu.make_async_remote_copy(
                src_ref=source,
                dst_ref=buffer.at[me],
                send_sem=sends.at[step],
                recv_sem=recvs.at[me],
                device_id=device(lax.rem(me + step, count)),
                device_id_type=mesh_id,
            )
            copy.start()
            copies.append(copy)
        buffer[me] = source[...]
        for step in range(1, count):
            other = lax.rem(me + step, count)
            pltpu.make_async_remote_copy(
                src_ref=source,
                dst_ref=buffer.at[other],
                send_sem=sends.at[step],
                recv_sem=recvs.at[other],
                device_id=device(other),
                device_id_type=mesh_id,
            ).wait_recv()
        for copy in copies:
            copy.wait_send()
        total = buffer[0]
        for other in range(1, count):
            total = total + buffer[other]
        return total

    total = reduce(row_count, my_row, lambda d: (d, my_col), part, red_row, send_r, recv_r)
    part2 = red_col.at[col_count]
    part2[...] = total
    total = reduce(col_count, my_col, lambda d: (my_row, d), part2, red_col, send_c, recv_c)
    pixels = rows * cols * row_count * col_count
    for m in range(MS):
        strength[m] = jnp.sum(total[m : m + 1, :]) / pixels

    for m in range(MS):
        each_around(lambda k, m=m: fresh_copy(m, k).wait_send())
    each_around(lambda k: comp_pair(k, True).wait_send())


def shards(slc_stack, land_mask):
    rows, cols = land_mask.shape
    row_count, col_count = lax.axis_size("row"), lax.axis_size("col")
    f32, bf16 = jnp.float32, jnp.bfloat16
    images = (MS, SLOTS * 2 * rows, cols)
    fresh_count = len(FRESH) * 2 * SUB
    comp_count = 2 * SUB * (-(-(M + 1) // SUB))
    vmem = pl.BlockSpec(memory_space=pltpu.VMEM)
    dma = pltpu.SemaphoreType.DMA
    return pl.pallas_call(
        functools.partial(kernel, row_count, col_count),
        out_shape=(
            jax.ShapeDtypeStruct(slc_stack.shape, f32),
            jax.ShapeDtypeStruct((2, rows, cols), f32),
            jax.ShapeDtypeStruct((MS,), f32),
        ),
        in_specs=[vmem, vmem],
        out_specs=(vmem, vmem, pl.BlockSpec(memory_space=pltpu.SMEM)),
        scratch_shapes=[
            pltpu.VMEM(images, f32),
            pltpu.VMEM(images, f32),
            pltpu.VMEM(images, f32),
            pltpu.VMEM((MS, 2, HALO_ROWS, cols), f32),
            pltpu.VMEM((MS, 6, HALO_ROOM, cols), f32),
            pltpu.VMEM((MS, 2, HALO_ROOM, cols), f32),
            pltpu.VMEM((2 * rows, cols), f32),
            pltpu.VMEM((2 * rows, cols), f32),
            pltpu.VMEM((2 * rows, cols), f32),
            pltpu.VMEM((2, SUB, cols), f32),
            pltpu.VMEM((6, SUB, cols), f32),
            pltpu.VMEM((2 * cols, cols), bf16),
            pltpu.VMEM((2 * cols, rows * cols), bf16),
            pltpu.VMEM((rows, fresh_count, 2 * cols), bf16),
            pltpu.VMEM((2, fresh_count, 2 * cols), bf16),
            pltpu.VMEM((rows * fresh_count, cols), f32),
            pltpu.VMEM((rows, comp_count, 2 * cols), bf16),
            pltpu.VMEM((2, comp_count, 2 * cols), bf16),
            pltpu.VMEM((rows * comp_count, cols), f32),
            pltpu.VMEM(((M + 1) * (M + 1), rows, cols), f32),
            pltpu.VMEM((SUB, cols), f32),
            pltpu.VMEM((row_count, SUB, cols), f32),
            pltpu.VMEM((col_count + 1, SUB, cols), f32),
            dma((MS, len(AROUND))),
            dma((MS, len(AROUND))),
            dma((len(AROUND),)),
            dma((len(AROUND),)),
            dma((row_count,)),
            dma((row_count,)),
            dma((col_count,)),
            dma((col_count,)),
        ],
        compiler_params=pltpu.CompilerParams(collective_id=0, has_side_effects=True),
        name="linker",
    )(slc_stack, land_mask)


def solution(mesh):
    return jax.shard_map(
        shards,
        mesh=mesh,
        in_specs=(P(None, None, "row", "col"), P("row", "col")),
        out_specs=(P(None, None, "row", "col"), P(None, "row", "col"), P()),
        check_vma=False,
    )
```

profile of v0, /device:TPU:0, one launch (start us, length us, event | category | flops | bytes accessed | tf_op | source)
XLA Modules:
  0.0 28.7 jit_solution(7389185315091513869)
XLA Ops:
  0.6 25.3 %linker.1 = (f32[20,2,8,128]{3,2,1,0:T(8,128)}, f32[2,8,128]{2,1,0:T(8,128)}, f32[2]{0:T(128)}) custom-call(f32[20,2,8,128]{3,2,1,0:T(8,128)} %slc.1, s32[8,128]{1,0:T(8,128)} %land.1), custom_call_target="tpu_custom_call" | custom-call | tf_op jit(solution)/shard_map/linker/pallas_call | solution.py:568
  25.9 0.0 copy-start
  26.0 1.6 %copy.8 = f32[20,2,8,128]{3,2,1,0:T(8,128)} copy(f32[20,2,8,128]{3,2,1,0:T(8,128)} %get-tuple-element.6) | data formatting | bytes 327680
  27.6 0.0 copy-done
  27.6 0.0 copy-start.1
  27.6 0.6 %copy.9 = f32[2,8,128]{2,1,0:T(8,128)} copy(f32[2,8,128]{2,1,0:T(8,128)S(1)} %copy-done) | data formatting | bytes 16384
  28.2 0.0 copy-done.1
  28.2 0.5 %copy.10 = f32[2]{0:T(128)} copy(f32[2]{0:T(128)S(1)} %copy-done.1) | data formatting | bytes 16
Async XLA Ops:
  25.9 1.6 %copy-start = (f32[2,8,128]{2,1,0:T(8,128)S(1)}, f32[2,8,128]{2,1,0:T(8,128)}, u32[]{:S(2)}) copy-start(f32[2,8,128]{2,1,0:T(8,128)} %get-tuple-element.7) | copy-start | bytes 24580
  27.6 0.6 %copy-start.1 = (f32[2]{0:T(128)S(1)}, f32[2]{0:T(128)}, u32[]{:S(2)}) copy-start(f32[2]{0:T(128)} %get-tuple-element.8) | copy-start | bytes 28
where the time goes:
time: 28.8 us; the launch traced here: 28.7 us
  Pallas kernels  25.3 us (88%)
  local copies, waits for them, and re-layouts  2.72 us (9%)
  between operations  0.65 us (2%)
    pallas_call x1, Pallas kernels, shards(): pl.pallas_call(functools.partial(kernel, row_count, col_count), out_shape...  25.3 us
    unnamed x7, local copies, waits for them, and re-layouts  2.72 us

commit v1 on v0

--- a/solution.py
+++ b/solution.py
@@ -71,11 +71,14 @@
 def kernel(
     row_count,
     col_count,
-    slc,
-    land,
+    direct,
+    slc_hbm,
+    land_hbm,
     linked,
     comp_out,
     strength,
+    slc,
+    land,
     sig,
     up,
     dn,
@@ -99,6 +102,8 @@
     part,
     red_row,
     red_col,
+    load_sem,
+    ready,
     send_a,
     recv_a,
     send_b,
@@ -112,6 +117,12 @@
     my_row = lax.axis_index("row")
     my_col = lax.axis_index("col")
     strip = rows * REACH
+    loads = [
+        pltpu.make_async_copy(slc_hbm, slc, load_sem.at[0]),
+        pltpu.make_async_copy(land_hbm, land, load_sem.at[1]),
+    ]
+    for load in loads:
+        load.start()
 
     exists = []
     for dr, dc in AROUND:
@@ -158,6 +169,8 @@
 
             expected = expected + exists[k].astype(jnp.int32)
 
+    for load in loads:
+        load.wait()
     mask = land[...].astype(jnp.float32)
     for m in range(MS):
         for i in range(M):
@@ -247,6 +260,12 @@
 
     for m in range(MS):
         each_around(lambda k, m=m: fresh_copy(m, k).start())
+
+    if direct:
+        for step in range(1, col_count):
+            pl.semaphore_signal(
+                ready, inc=1, device_id=(my_row, lax.rem(my_col + step, col_count)), device_id_type=mesh_id
+            )
 
     k_at = lax.broadcasted_iota(jnp.int32, (cols, cols), 0)
     n_at = lax.broadcasted_iota(jnp.int32, (cols, cols), 1)
@@ -416,7 +435,13 @@
             comp_im = y if comp_im is None else comp_im + y
             linked[m * M + i, 0] = re[i] * mask
             linked[m * M + i, 1] = im[i] * mask
-        part[m : m + 1, :] = jnp.sum(mask * length, axis=0, keepdims=True) * (1.0 / number)
+        share = jnp.sum(mask * length, axis=0, keepdims=True) * (1.0 / number)
+        share = share + pltpu.roll(share, cols // 2, 1)
+        lane_line = lax.broadcasted_iota(jnp.int32, (1, cols), 1)
+        if m == 0:
+            part[...] = share
+        else:
+            part[...] = jnp.where(lane_line < cols // 2, part[...], share)
         return comp_re, comp_im
 
     def take_fresh(m):
@@ -507,7 +532,6 @@
         at = (other // SUB) * 2 * SUB + p * SUB + other % SUB
         return zcbuf[pl.ds(at, rows, stride=comp_count), :]
 
-    part[...] = jnp.where(lax.broadcasted_iota(jnp.int32, part.shape, 0) < 1, part[...], 0.0)
     comp_re, comp_im = finish(last, M + 1, last_field)
     comp_out[0] = comp_re
     comp_out[1] = comp_im
@@ -543,17 +567,37 @@
             total = total + buffer[other]
         return total
 
-    total = reduce(row_count, my_row, lambda d: (d, my_col), part, red_row, send_r, recv_r)
-    part2 = red_col.at[col_count]
-    part2[...] = total
-    total = reduce(col_count, my_col, lambda d: (my_row, d), part2, red_col, send_c, recv_c)
-    pixels = rows * cols * row_count * col_count
-    for m in range(MS):
-        strength[m] = jnp.sum(total[m : m + 1, :]) / pixels
+    if direct:
+        pl.semaphore_wait(ready, col_count - 1)
+        me = my_row * col_count + my_col
+        total = reduce(
+            row_count * col_count, me, lambda d: (d // col_count, d % col_count), part, red_row, send_r, recv_r
+        )
+    else:
+        total = reduce(row_count, my_row, lambda d: (d, my_col), part, red_row, send_r, recv_r)
+        part2 = red_col.at[col_count]
+        part2[...] = total
+        total = reduce(col_count, my_col, lambda d: (my_row, d), part2, red_col, send_c, recv_c)
+    strength[...] = total
 
     for m in range(MS):
         each_around(lambda k, m=m: fresh_copy(m, k).wait_send())
     each_around(lambda k: comp_pair(k, True).wait_send())
+
+
+def closing(pixels, linked_in, comp_in, total, linked, comp, strength, sems):
+    copies = [
+        pltpu.make_async_copy(linked_in, linked, sems.at[0]),
+        pltpu.make_async_copy(comp_in, comp, sems.at[1]),
+    ]
+    for copy in copies:
+        copy.start()
+    for m in range(MS):
+        lane = lax.broadcasted_iota(jnp.int32, total.shape, 1)
+        mine = lane < total.shape[1] // 2 if m == 0 else lane >= total.shape[1] // 2
+        strength[m] = jnp.sum(jnp.where(mine, total[...], 0.0)) / pixels
+    for copy in copies:
+        copy.wait()
 
 
 def shards(slc_stack, land_mask):
@@ -565,16 +609,20 @@
     comp_count = 2 * SUB * (-(-(M + 1) // SUB))
     vmem = pl.BlockSpec(memory_space=pltpu.VMEM)
     dma = pltpu.SemaphoreType.DMA
-    return pl.pallas_call(
-        functools.partial(kernel, row_count, col_count),
-        out_shape=(
-            jax.ShapeDtypeStruct(slc_stack.shape, f32),
-            jax.ShapeDtypeStruct((2, rows, cols), f32),
-            jax.ShapeDtypeStruct((MS,), f32),
-        ),
-        in_specs=[vmem, vmem],
-        out_specs=(vmem, vmem, pl.BlockSpec(memory_space=pltpu.SMEM)),
+    hbm = pl.BlockSpec(memory_space=pltpu.HBM)
+    devices = row_count * col_count
+    direct = devices <= 64
+    peers = devices if direct else row_count
+    linked_shape = jax.ShapeDtypeStruct(slc_stack.shape, f32)
+    comp_shape = jax.ShapeDtypeStruct((2, rows, cols), f32)
+    linked, comp, total = pl.pallas_call(
+        functools.partial(kernel, row_count, col_count, direct),
+        out_shape=(linked_shape, comp_shape, jax.ShapeDtypeStruct((1, cols), f32)),
+        in_specs=[hbm, hbm],
+        out_specs=(vmem, vmem, vmem),
         scratch_shapes=[
+            pltpu.VMEM(slc_stack.shape, f32),
+            pltpu.VMEM((rows, cols), jnp.int32),
             pltpu.VMEM(images, f32),
             pltpu.VMEM(images, f32),
             pltpu.VMEM(images, f32),
@@ -595,21 +643,32 @@
             pltpu.VMEM((2, comp_count, 2 * cols), bf16),
             pltpu.VMEM((rows * comp_count, cols), f32),
             pltpu.VMEM(((M + 1) * (M + 1), rows, cols), f32),
-            pltpu.VMEM((SUB, cols), f32),
-            pltpu.VMEM((row_count, SUB, cols), f32),
-            pltpu.VMEM((col_count + 1, SUB, cols), f32),
+            pltpu.VMEM((1, cols), f32),
+            pltpu.VMEM((peers, 1, cols), f32),
+            pltpu.VMEM((col_count + 1, 1, cols), f32),
+            dma((2,)),
+            pltpu.SemaphoreType.REGULAR,
             dma((MS, len(AROUND))),
             dma((MS, len(AROUND))),
             dma((len(AROUND),)),
             dma((len(AROUND),)),
-            dma((row_count,)),
-            dma((row_count,)),
+            dma((peers,)),
+            dma((peers,)),
             dma((col_count,)),
             dma((col_count,)),
         ],
-        compiler_params=pltpu.CompilerParams(collective_id=0, has_side_effects=True),
+        compiler_params=pltpu.CompilerParams(collective_id=0, has_side_effects=True, vmem_limit_bytes=16 << 20),
         name="linker",
-    )(slc_stack, land_mask)
+    )(*(pltpu.with_memory_space_constraint(x, pltpu.HBM) for x in (slc_stack, land_mask)))
+    return pl.pallas_call(
+        functools.partial(closing, rows * cols * devices),
+        out_shape=(linked_shape, comp_shape, jax.ShapeDtypeStruct((MS,), f32)),
+        in_specs=[vmem, vmem, vmem],
+        out_specs=(hbm, hbm, pl.BlockSpec(memory_space=pltpu.SMEM)),
+        scratch_shapes=[dma((2,))],
+        compiler_params=pltpu.CompilerParams(vmem_limit_bytes=4 << 20),
+        name="closing",
+    )(linked, comp, total)
 
 
 def solution(mesh):

time: 28.8 us -> 24 us (0.83)
  local copies, waits for them, and re-layouts: 2.72 us -> 0 us
  Pallas kernels: 25.3 us -> 23.2 us
    unnamed x7 -> x0, local copies, waits for them, and re-layouts: 2.72 us -> none
    pallas_call x1 -> x2, Pallas kernels: 25.3 us -> 23.2 us  [the longest x1 22 us: shards(): pl.pallas_call(functools.partial(kernel, row_count, col_count, direct), o...]
where the time goes in v1:
time: 24 us; the launch traced here: 23.9 us
  Pallas kernels  23.2 us (97%)
  between operations  0.64 us (3%)
    pallas_call x1, Pallas kernels, shards(): pl.pallas_call(functools.partial(kernel, row_count, col_count, direct), o...  22 us
    pallas_call x1, Pallas kernels, shards(): pl.pallas_call(functools.partial(closing, rows * cols * devices), out_sha...  1.2 us

profile of v1, /device:TPU:0, one launch (start us, length us, event | category | flops | bytes accessed | tf_op | source)
XLA Modules:
  0.0 23.9 jit_solution(5366835162707014717)
XLA Ops:
  0.6 22.0 %linker.1 = (f32[20,2,8,128]{3,2,1,0:T(8,128)S(1)}, f32[2,8,128]{2,1,0:T(8,128)S(1)}, f32[1,128]{1,0:T(1,128)S(1)}) custom-call(f32[20,2,8,128]{3,2,1,0:T(8,128)} %slc_hbm.1, s32[8,128]{1,0:T(8,128)} %land_hbm.1), custom_call_target="tpu_custom_call" | custom-call | tf_op jit(solution)/shard_map/linker/pallas_call | solution.py:618
  22.7 1.2 %closing.1 = (f32[20,2,8,128]{3,2,1,0:T(8,128)}, f32[2,8,128]{2,1,0:T(8,128)}, f32[2]{0:T(128)}) custom-call(f32[20,2,8,128]{3,2,1,0:T(8,128)S(1)} %get-tuple-element.6.linked_in, f32[2,8,128]{2,1,0:T(8,128)S(1)} %get-tuple-element.7.comp_in, f32[1,128]{1,0:T(1,128)S(1)} %get-tuple-element.8.total), custom_call_target="tpu_custom_call" | custom-call | tf_op jit(solution)/shard_map/closing/pallas_call | solution.py:663
